TPU v7x, 32 devices: a whole 2x2x4 slice. The times are simulated.
32 devices in a mesh: rows: 8 (over z, y), grp: 4 (over x, core).
Axes of the slice: x: 2, y: 2, z: 4, core: 2. Of those that a mesh axis runs over, the one named last changes fastest.
Arguments:
- basis: float32 [32, 65536], P(None, ('rows', 'grp')), may hold values from -0.03125 to 0.03125, as said below
- core: float32 [32, 32], replicated, may hold values from -0.3 to 4
- snapshots: bfloat16 [4, 32, 65536], P(None, 'grp', 'rows'), may hold values from -16 to 16
Outputs:
- new_basis: float32 [32, 65536], P(None, ('rows', 'grp'))
- new_core: float32 [32, 32], replicated
- first_coeffs: float32 [4, 32, 32], replicated
Inputs may be any that keep to these rules, and one draw needn't show every extreme that they name: `basis`: rows orthonormal up to float32 rounding.
All inputs are finite; a program needn't handle non-finite values.
Results may differ from a plain program's by a relative error of at most 0.0003.
Values may be sent and summed in bfloat16 or wider, within the bound.
A program may use at most 64 MiB of HBM per device.

v0:
```python
import jax
import jax.numpy as jnp
from jax import lax
from jax.sharding import PartitionSpec as P

BATCHES = 4
epsilon = 1e-06


def contract_rows(left, right):
    return lax.dot_general(
        left,
        right,
        (((1,), (1,)), ((), ())),
        precision=lax.Precision.HIGHEST,
        preferred_element_type=jnp.float32,
    )


def matmul(left, right):
    return jnp.dot(left, right, precision=lax.Precision.HIGHEST, preferred_element_type=jnp.float32)


def lower_solve(factor, right):
    return lax.linalg.triangular_solve(factor, right, left_side=True, lower=True)


def small_update(core_now, total, lower):
    rank = core_now.shape[0]
    cols = lower.shape[0]
    top = jnp.concatenate([core_now, total], axis=1)
    bottom = jnp.concatenate([jnp.zeros((cols, rank), jnp.float32), lower.T], axis=1)
    stacked = jnp.concatenate([top, bottom], axis=0)
    moment = matmul(stacked, stacked.T)
    leading = moment[:, :rank]
    factor = jnp.linalg.cholesky(matmul(leading.T, leading))
    rotation = lower_solve(factor, leading.T).T
    fresh_core = jnp.linalg.cholesky(matmul(rotation.T, matmul(moment, rotation)))
    return (rotation, fresh_core)


def body(basis, core, snapshots):
    rank = basis.shape[0]
    basis_now = basis
    core_now = core
    firsts = []
    gram_basis = lax.psum(contract_rows(basis_now, basis_now), ("rows", "grp"))
    for batch in range(BATCHES):
        columns = lax.all_to_all(snapshots[batch], "grp", split_axis=1, concat_axis=0, tiled=True)
        raw = columns.astype(jnp.float32)
        raw_cross, raw_gram = lax.psum(
            (contract_rows(basis_now, raw), contract_rows(raw, raw)), ("rows", "grp")
        )
        inverse = lax.rsqrt(jnp.diagonal(raw_gram) + epsilon)
        scaled = raw * inverse[:, None]
        cross = raw_cross * inverse[None, :]
        gram_raw = raw_gram * inverse[:, None] * inverse[None, :]
        second = cross - matmul(gram_basis, cross)
        total = cross + second
        basis_cross = cross - matmul(gram_basis, total)
        gram = (
            gram_raw
            - matmul(total.T, cross)
            - matmul(cross.T, total)
            + matmul(total.T, matmul(gram_basis, total))
        )
        twice = scaled - matmul(total.T, basis_now)
        lower = jnp.linalg.cholesky(gram)
        fresh = lower_solve(lower, twice)
        rotation, core_now = small_update(core_now, total, lower)
        cross_fresh = lower_solve(lower, basis_cross.T).T
        halfway = lower_solve(lower, gram)
        gram_fresh = lower_solve(lower, halfway.T).T
        upper_block = jnp.concatenate([gram_basis, cross_fresh], axis=1)
        lower_block = jnp.concatenate([cross_fresh.T, gram_fresh], axis=1)
        combined = jnp.concatenate([upper_block, lower_block], axis=0)
        gram_basis = matmul(rotation.T, matmul(combined, rotation))
        firsts.append(cross)
        basis_now = matmul(rotation[:rank].T, basis_now) + matmul(rotation[rank:].T, fresh)
    return (basis_now, core_now, jnp.stack(firsts, axis=0))


def solution(mesh):
    return jax.shard_map(
        body,
        mesh=mesh,
        in_specs=(P(None, ("rows", "grp")), P(), P(None, "grp", "rows")),
        out_specs=(P(None, ("rows", "grp")), P(), P()),
        check_vma=False,
    )
```

profile of v0, /device:TPU:0, one launch (start us, length us, event | category | flops | bytes accessed | tf_op | source)
XLA Modules:
  0.0 283.6 jit_solution(1562950860485663812)
XLA Ops:
  0.6 1.9 fusion.229
  2.6 4.4 %all-to-all-start = ((bf16[8,4,2048]{2,0,1:T(8,128)(2,1)}), bf16[8,4,2048]{2,0,1:T(8,128)(2,1)S(1)}, u32[]{:S(2)}, u32[]{:S(2)}) async-start(bf16[8,4,2048]{2,0,1:T(8,128)(2,1)} %bitcast), calls=%async_computation | async-start | bytes 262144 | tf_op jit(solution)/shard_map/all_to_all | solution.py:49
  7.4 4.1 %all-to-all-done = bf16[8,4,2048]{2,0,1:T(8,128)(2,1)S(1)} async-done(((bf16[8,4,2048]{2,0,1:T(8,128)(2,1)}), bf16[8,4,2048]{2,0,1:T(8,128)(2,1)S(1)}, u32[]{:S(2)}, u32[]{:S(2)}) %all-to-all-start) | async-done | bytes 131104 | tf_op jit(solution)/shard_map/all_to_all | solution.py:49
  11.6 3.3 %all-to-all-start.1 = ((bf16[8,4,2048]{2,0,1:T(8,128)(2,1)}), bf16[8,4,2048]{2,0,1:T(8,128)(2,1)S(1)}, u32[]{:S(2)}, u32[]{:S(2)}) async-start(bf16[8,4,2048]{2,0,1:T(8,128)(2,1)} %bitcast.15), calls=%async_computation.1 | async-start | bytes 262144 | tf_op jit(solution)/shard_map/all_to_all | solution.py:49
  15.3 42.1 %all-reduce.7 = (f32[32,32]{1,0:T(8,128)S(1)}, f32[32,32]{0,1:T(8,128)S(1)}, f32[32,32]{0,1:T(8,128)S(1)}) all-reduce(f32[32,32]{1,0:T(8,128)S(1)} %fusion.230, f32[32,32]{0,1:T(8,128)S(1)} %fusion.18, f32[32,32]{0,1:T(8,128)S(1)} %fusion.16), channel_id=1, replica_groups=mesh['rows'=8,'grp'=4] {'rows','grp'}, use_global_device_ids=true, to_apply=%region_2.0 | all-reduce | flops 3072 | bytes 24576 | tf_op jit(solution)/shard_map/psum | solution.py:47
  57.4 0.7 gather_fusion
  59.3 2.9 %cholesky.194 = f32[32,32]{1,0:T(8,128)S(1)} custom-call(f32[32,32]{1,0:T(8,128)S(1)} %fusion.134), custom_call_target="Cholesky" | custom-call | tf_op jit(solution)/shard_map/jit(cholesky)/cholesky | solution.py:68
  62.9 0.7 fusion.143
  63.6 2.4 custom-call.34
  67.2 2.9 %cholesky.205 = f32[32,32]{1,0:T(8,128)S(1)} custom-call(f32[32,32]{1,0:T(8,128)S(1)} %fusion.133), custom_call_target="Cholesky" | custom-call | tf_op jit(solution)/shard_map/jit(cholesky)/cholesky | solution.py:36
  70.8 0.7 fusion.64
  71.4 2.4 custom-call.33
  76.5 3.5 %all-to-all-start.2 = ((bf16[8,4,2048]{2,0,1:T(8,128)(2,1)}), bf16[8,4,2048]{2,0,1:T(8,128)(2,1)S(1)}, u32[]{:S(2)}, u32[]{:S(2)}) async-start(bf16[8,4,2048]{2,0,1:T(8,128)(2,1)} %bitcast.39), calls=%async_computation.2 | async-start | bytes 262144 | tf_op jit(solution)/shard_map/all_to_all | solution.py:49
  80.4 41.5 %all-reduce.6 = (f32[32,32]{0,1:T(8,128)S(1)}, f32[32,32]{0,1:T(8,128)S(1)}) all-reduce(f32[32,32]{0,1:T(8,128)S(1)} %fusion.14, f32[32,32]{0,1:T(8,128)S(1)} %fusion.12), channel_id=1, replica_groups=mesh['rows'=8,'grp'=4] {'rows','grp'}, use_global_device_ids=true, to_apply=%region_5.9 | all-reduce | flops 2048 | bytes 16384 | tf_op jit(solution)/shard_map/psum | solution.py:51
  121.9 0.7 gather_fusion.1
  123.5 2.9 %cholesky.216 = f32[32,32]{1,0:T(8,128)S(1)} custom-call(f32[32,32]{1,0:T(8,128)S(1)} %fusion.129), custom_call_target="Cholesky" | custom-call | tf_op jit(solution)/shard_map/jit(cholesky)/cholesky | solution.py:38
  127.3 0.6 fusion.163
  128.5 2.9 %cholesky.227 = f32[32,32]{1,0:T(8,128)S(1)} custom-call(f32[32,32]{1,0:T(8,128)S(1)} %fusion.121), custom_call_target="Cholesky" | custom-call | tf_op jit(solution)/shard_map/jit(cholesky)/cholesky | solution.py:68
  132.1 0.7 fusion.144
  132.8 2.4 custom-call.39
  136.4 2.9 %cholesky.238 = f32[32,32]{1,0:T(8,128)S(1)} custom-call(f32[32,32]{1,0:T(8,128)S(1)} %fusion.120), custom_call_target="Cholesky" | custom-call | tf_op jit(solution)/shard_map/jit(cholesky)/cholesky | solution.py:36
  140.0 0.7 fusion.65
  140.7 2.4 custom-call.38
  145.7 3.5 %all-to-all-start.3 = ((bf16[8,4,2048]{2,0,1:T(8,128)(2,1)}), bf16[8,4,2048]{2,0,1:T(8,128)(2,1)S(1)}, u32[]{:S(2)}, u32[]{:S(2)}) async-start(bf16[8,4,2048]{2,0,1:T(8,128)(2,1)} %bitcast.63), calls=%async_computation.3 | async-start | bytes 262144 | tf_op jit(solution)/shard_map/all_to_all | solution.py:49
  149.7 40.7 %all-reduce.5 = (f32[32,32]{0,1:T(8,128)S(1)}, f32[32,32]{0,1:T(8,128)S(1)}) all-reduce(f32[32,32]{0,1:T(8,128)S(1)} %fusion.10, f32[32,32]{0,1:T(8,128)S(1)} %fusion.8), channel_id=1, replica_groups=mesh['rows'=8,'grp'=4] {'rows','grp'}, use_global_device_ids=true, to_apply=%region_7.12 | all-reduce | flops 2048 | bytes 16384 | tf_op jit(solution)/shard_map/psum | solution.py:51
  190.4 0.7 gather_fusion.2
  192.0 2.9 %cholesky.249 = f32[32,32]{1,0:T(8,128)S(1)} custom-call(f32[32,32]{1,0:T(8,128)S(1)} %fusion.116), custom_call_target="Cholesky" | custom-call | tf_op jit(solution)/shard_map/jit(cholesky)/cholesky | solution.py:38
  195.7 0.6 fusion.164
  197.0 2.9 %cholesky.260 = f32[32,32]{1,0:T(8,128)S(1)} custom-call(f32[32,32]{1,0:T(8,128)S(1)} %fusion.108), custom_call_target="Cholesky" | custom-call | tf_op jit(solution)/shard_map/jit(cholesky)/cholesky | solution.py:68
  200.6 0.7 fusion.142
  201.2 2.4 custom-call.44
  204.8 2.9 %cholesky.271 = f32[32,32]{1,0:T(8,128)S(1)} custom-call(f32[32,32]{1,0:T(8,128)S(1)} %fusion.107), custom_call_target="Cholesky" | custom-call | tf_op jit(solution)/shard_map/jit(cholesky)/cholesky | solution.py:36
  208.5 0.7 fusion.66
  209.1 2.4 custom-call.43
  214.6 39.8 %all-reduce.4 = (f32[32,32]{0,1:T(8,128)S(1)}, f32[32,32]{0,1:T(8,128)S(1)}) all-reduce(f32[32,32]{0,1:T(8,128)S(1)} %fusion.6, f32[32,32]{0,1:T(8,128)S(1)} %fusion.4), channel_id=1, replica_groups=mesh['rows'=8,'grp'=4] {'rows','grp'}, use_global_device_ids=true, to_apply=%region_9.14 | all-reduce | flops 2048 | bytes 16384 | tf_op jit(solution)/shard_map/psum | solution.py:51
  254.5 0.7 gather_fusion.3
  256.1 2.9 %cholesky.282 = f32[32,32]{1,0:T(8,128)S(1)} custom-call(f32[32,32]{1,0:T(8,128)S(1)} %fusion.103), custom_call_target="Cholesky" | custom-call | tf_op jit(solution)/shard_map/jit(cholesky)/cholesky | solution.py:38
  259.9 0.6 select_select_fusion.5
  260.8 0.7 copy.105
  261.8 2.9 %cholesky.293 = f32[32,32]{1,0:T(8,128)S(1)} custom-call(f32[32,32]{1,0:T(8,128)S(1)} %fusion.95), custom_call_target="Cholesky" | custom-call | tf_op jit(solution)/shard_map/jit(cholesky)/cholesky | solution.py:68
  265.4 0.7 select_bitcast_fusion
  266.0 2.4 custom-call.49
  269.0 2.9 %cholesky.304 = f32[32,32]{1,0:T(8,128)S(1)} custom-call(f32[32,32]{1,0:T(8,128)S(1)} %fusion.94), custom_call_target="Cholesky" | custom-call | tf_op jit(solution)/shard_map/jit(cholesky)/cholesky | solution.py:36
  272.6 0.7 fusion.67
  273.3 2.4 custom-call.48
  276.5 2.9 %cholesky.315 = f32[32,32]{1,0:T(8,128)S(1)} custom-call(f32[32,32]{1,0:T(8,128)S(1)} %fusion.88), custom_call_target="Cholesky" | custom-call | tf_op jit(solution)/shard_map/jit(cholesky)/cholesky | solution.py:38
  280.1 1.3 select_select_fusion.4
  282.5 1.1 convolution_add_fusion
  (154 shorter events, 29.5 us)
Async XLA Ops:
  0.6 6.4 %copy-start = (f32[32,2048]{1,0:T(8,128)S(1)}, f32[32,2048]{1,0:T(8,128)}, u32[]{:S(2)}) copy-start(f32[32,2048]{1,0:T(8,128)} %param.10) | copy-start | bytes 786436
  2.6 4.4 %copy-start.1 = (f32[32,32]{1,0:T(8,128)S(1)}, f32[32,32]{1,0:T(8,128)}, u32[]{:S(2)}) copy-start(f32[32,32]{1,0:T(8,128)} %param.11) | copy-start | bytes 12292
  2.6 9.0 %all-to-all-start = ((bf16[8,4,2048]{2,0,1:T(8,128)(2,1)}), bf16[8,4,2048]{2,0,1:T(8,128)(2,1)S(1)}, u32[]{:S(2)}, u32[]{:S(2)}) async-start(bf16[8,4,2048]{2,0,1:T(8,128)(2,1)} %bitcast), calls=%async_computation | async-start | bytes 262144 | tf_op jit(solution)/shard_map/all_to_all | solution.py:49
  11.6 64.9 %all-to-all-start.1 = ((bf16[8,4,2048]{2,0,1:T(8,128)(2,1)}), bf16[8,4,2048]{2,0,1:T(8,128)(2,1)S(1)}, u32[]{:S(2)}, u32[]{:S(2)}) async-start(bf16[8,4,2048]{2,0,1:T(8,128)(2,1)} %bitcast.15), calls=%async_computation.1 | async-start | bytes 262144 | tf_op jit(solution)/shard_map/all_to_all | solution.py:49
  76.5 69.2 %all-to-all-start.2 = ((bf16[8,4,2048]{2,0,1:T(8,128)(2,1)}), bf16[8,4,2048]{2,0,1:T(8,128)(2,1)S(1)}, u32[]{:S(2)}, u32[]{:S(2)}) async-start(bf16[8,4,2048]{2,0,1:T(8,128)(2,1)} %bitcast.39), calls=%async_computation.2 | async-start | bytes 262144 | tf_op jit(solution)/shard_map/all_to_all | solution.py:49
  145.7 68.5 %all-to-all-start.3 = ((bf16[8,4,2048]{2,0,1:T(8,128)(2,1)}), bf16[8,4,2048]{2,0,1:T(8,128)(2,1)S(1)}, u32[]{:S(2)}, u32[]{:S(2)}) async-start(bf16[8,4,2048]{2,0,1:T(8,128)(2,1)} %bitcast.63), calls=%async_computation.3 | async-start | bytes 262144 | tf_op jit(solution)/shard_map/all_to_all | solution.py:49
where the time goes:
time: 285 us; the launch traced here: 284 us
  blocking collectives  164 us (58%)
  other arithmetic  71.8 us (25%)
  matrix products  20.3 us (7%)
  starting transfers between devices  14.7 us (5%)
  local copies, waits for them, and re-layouts  7.12 us (2%)
  waiting for transfers between devices  4.15 us (1%)
    psum x3, blocking collectives, body(): lax.psum((contract_rows(basis_now, raw), contract_rows(raw, raw)), ('rows...  122 us
    psum x1, blocking collectives, body(): gram_basis = lax.psum(contract_rows(basis_now, basis_now), ('rows', 'grp'))  42.1 us
    another operation x16, other arithmetic, lower_solve(): lax.linalg.triangular_solve(factor, right, left_side=True, lower=True)  24.7 us
    all_to_all x4, starting transfers between devices, body(): lax.all_to_all(snapshots[batch], 'grp', split_axis=1, concat_axis=0, tile...  14.7 us
    another operation x12, other arithmetic, small_update(): jnp.linalg.cholesky(matmul(rotation.T, matmul(moment, rotation)))  14.7 us
    another operation x12, other arithmetic, small_update(): factor = jnp.linalg.cholesky(matmul(leading.T, leading))  14.4 us
    another operation x12, other arithmetic, body(): lower = jnp.linalg.cholesky(gram)  14.4 us
    dot_general x54, matrix products, matmul(): jnp.dot(left, right, precision=lax.Precision.HIGHEST, preferred_element_t...  13.7 us
  transfers between devices with their start and end apart: 4, of which 1 were waited for; matrix products, arithmetic and copies ran while one was open for 24% of the time, Pallas kernels for 0%

commit v1 on v0

--- a/solution.py
+++ b/solution.py
@@ -44,7 +44,7 @@
     basis_now = basis
     core_now = core
     firsts = []
-    gram_basis = lax.psum(contract_rows(basis_now, basis_now), ("rows", "grp"))
+    gram_basis = lax.psum(lax.psum(contract_rows(basis_now, basis_now), "grp"), "rows")
     for batch in range(BATCHES):
         columns = lax.all_to_all(snapshots[batch], "grp", split_axis=1, concat_axis=0, tiled=True)
         raw = columns.astype(jnp.float32)

time: 285 us -> 327 us (1.15)
  blocking collectives: 164 us -> 210 us
  waiting for transfers between devices: 4.15 us -> 0.01 us
    psum x3 -> x4, blocking collectives: 122 us -> 161 us  [body(): lax.psum((contract_rows(basis_now, raw), contract_rows(raw, raw)), ('rows...]
    psum x1 -> x2, blocking collectives: 42.1 us -> 49.6 us  [the longest x1 37.9 us: body(): lax.psum(lax.psum(contract_rows(basis_now, basis_now), 'grp'), 'rows')]
    all_to_all x4, waiting for transfers between devices: 4.15 us -> 0.01 us  [body(): lax.all_to_all(snapshots[batch], 'grp', split_axis=1, concat_axis=0, tile...]
  transfers between devices with their start and end apart: 4 -> 4, of which waited for: 1 -> 0; matrix products, arithmetic and copies ran while one was open for 24% -> 21% of each run, Pallas kernels for 0% -> 0%
where the time goes in v1:
time: 327 us; the launch traced here: 326 us
  blocking collectives  210 us (64%)
  other arithmetic  71.8 us (22%)
  matrix products  20.2 us (6%)
  starting transfers between devices  14.8 us (5%)
  local copies, waits for them, and re-layouts  7.12 us (2%)
    psum x4, blocking collectives, body(): lax.psum((contract_rows(basis_now, raw), contract_rows(raw, raw)), ('rows...  161 us
    psum x1, blocking collectives, body(): lax.psum(lax.psum(contract_rows(basis_now, basis_now), 'grp'), 'rows')  37.9 us
    another operation x16, other arithmetic, lower_solve(): lax.linalg.triangular_solve(factor, right, left_side=True, lower=True)  24.7 us
    all_to_all x4, starting transfers between devices, body(): lax.all_to_all(snapshots[batch], 'grp', split_axis=1, concat_axis=0, tile...  14.8 us
    another operation x12, other arithmetic, small_update(): jnp.linalg.cholesky(matmul(rotation.T, matmul(moment, rotation)))  14.7 us
    another operation x12, other arithmetic, small_update(): factor = jnp.linalg.cholesky(matmul(leading.T, leading))  14.4 us
    another operation x12, other arithmetic, body(): lower = jnp.linalg.cholesky(gram)  14.4 us
    dot_general x54, matrix products, matmul(): jnp.dot(left, right, precision=lax.Precision.HIGHEST, preferred_element_t...  13.7 us
  transfers between devices with their start and end apart: 4, of which 0 were waited for; matrix products, arithmetic and copies ran while one was open for 21% of the time, Pallas kernels for 0%

profile of v1, /device:TPU:0, one launch (start us, length us, event | category | flops | bytes accessed | tf_op | source)
XLA Modules:
  0.0 325.5 jit_solution(11065912709965749365)
XLA Ops:
  0.6 1.9 fusion.229
  2.6 4.4 %all-to-all-start = ((bf16[8,4,2048]{2,0,1:T(8,128)(2,1)}), bf16[8,4,2048]{2,0,1:T(8,128)(2,1)S(1)}, u32[]{:S(2)}, u32[]{:S(2)}) async-start(bf16[8,4,2048]{2,0,1:T(8,128)(2,1)} %bitcast), calls=%async_computation | async-start | bytes 262144 | tf_op jit(solution)/shard_map/all_to_all | solution.py:49
  7.4 11.8 %psum.72 = f32[32,32]{1,0:T(8,128)S(1)} all-reduce(f32[32,32]{1,0:T(8,128)S(1)} %fusion.230), channel_id=1, replica_groups=mesh['rows'=8,'grp'=4] {'grp'}, use_global_device_ids=true, to_apply=%region_2.0 | all-reduce | flops 1024 | bytes 8192 | tf_op jit(solution)/shard_map/psum | solution.py:47
  19.1 37.9 %psum.73 = f32[32,32]{1,0:T(8,128)S(1)} all-reduce(f32[32,32]{1,0:T(8,128)S(1)} %psum.72), channel_id=1, replica_groups=mesh['rows'=8,'grp'=4] {'rows'}, use_global_device_ids=true, to_apply=%region_3.0 | all-reduce | flops 1024 | bytes 8192 | tf_op jit(solution)/shard_map/psum | solution.py:47
  57.0 3.3 %all-to-all-start.1 = ((bf16[8,4,2048]{2,0,1:T(8,128)(2,1)}), bf16[8,4,2048]{2,0,1:T(8,128)(2,1)S(1)}, u32[]{:S(2)}, u32[]{:S(2)}) async-start(bf16[8,4,2048]{2,0,1:T(8,128)(2,1)} %bitcast.15), calls=%async_computation.1 | async-start | bytes 262144 | tf_op jit(solution)/shard_map/all_to_all | solution.py:49
  60.8 37.2 %all-reduce.7 = (f32[32,32]{0,1:T(8,128)S(1)}, f32[32,32]{0,1:T(8,128)S(1)}) all-reduce(f32[32,32]{0,1:T(8,128)S(1)} %fusion.18, f32[32,32]{0,1:T(8,128)S(1)} %fusion.16), channel_id=1, replica_groups=mesh['rows'=8,'grp'=4] {'rows','grp'}, use_global_device_ids=true, to_apply=%region_0.0 | all-reduce | flops 2048 | bytes 16384 | tf_op jit(solution)/shard_map/psum | solution.py:51
  98.0 0.7 gather_fusion
  99.9 2.9 cholesky.194
  103.5 0.7 fusion.143
  104.2 2.4 custom-call.34
  107.8 2.9 cholesky.205
  111.4 0.7 fusion.64
  112.0 2.4 custom-call.33
  117.1 3.5 %all-to-all-start.2 = ((bf16[8,4,2048]{2,0,1:T(8,128)(2,1)}), bf16[8,4,2048]{2,0,1:T(8,128)(2,1)S(1)}, u32[]{:S(2)}, u32[]{:S(2)}) async-start(bf16[8,4,2048]{2,0,1:T(8,128)(2,1)} %bitcast.39), calls=%async_computation.2 | async-start | bytes 262144 | tf_op jit(solution)/shard_map/all_to_all | solution.py:49
  121.1 42.8 %all-reduce.6 = (f32[32,32]{0,1:T(8,128)S(1)}, f32[32,32]{0,1:T(8,128)S(1)}) all-reduce(f32[32,32]{0,1:T(8,128)S(1)} %fusion.14, f32[32,32]{0,1:T(8,128)S(1)} %fusion.12), channel_id=1, replica_groups=mesh['rows'=8,'grp'=4] {'rows','grp'}, use_global_device_ids=true, to_apply=%region_6.10 | all-reduce | flops 2048 | bytes 16384 | tf_op jit(solution)/shard_map/psum | solution.py:51
  163.9 0.7 gather_fusion.1
  165.5 2.9 cholesky.216
  169.2 0.6 fusion.163
  170.5 2.9 cholesky.227
  174.1 0.7 fusion.144
  174.7 2.4 custom-call.39
  178.3 2.9 cholesky.238
  182.0 0.7 fusion.65
  182.6 2.4 custom-call.38
  187.7 3.5 %all-to-all-start.3 = ((bf16[8,4,2048]{2,0,1:T(8,128)(2,1)}), bf16[8,4,2048]{2,0,1:T(8,128)(2,1)S(1)}, u32[]{:S(2)}, u32[]{:S(2)}) async-start(bf16[8,4,2048]{2,0,1:T(8,128)(2,1)} %bitcast.63), calls=%async_computation.3 | async-start | bytes 262144 | tf_op jit(solution)/shard_map/all_to_all | solution.py:49
  191.6 40.1 %all-reduce.5 = (f32[32,32]{0,1:T(8,128)S(1)}, f32[32,32]{0,1:T(8,128)S(1)}) all-reduce(f32[32,32]{0,1:T(8,128)S(1)} %fusion.10, f32[32,32]{0,1:T(8,128)S(1)} %fusion.8), channel_id=1, replica_groups=mesh['rows'=8,'grp'=4] {'rows','grp'}, use_global_device_ids=true, to_apply=%region_8.13 | all-reduce | flops 2048 | bytes 16384 | tf_op jit(solution)/shard_map/psum | solution.py:51
  231.7 0.7 gather_fusion.2
  233.3 2.9 cholesky.249
  238.3 2.9 cholesky.260
  241.9 0.7 fusion.142
  242.6 2.4 custom-call.44
  246.2 2.9 cholesky.271
  249.8 0.7 fusion.66
  250.4 2.4 custom-call.43
  255.9 40.5 %all-reduce.4 = (f32[32,32]{0,1:T(8,128)S(1)}, f32[32,32]{0,1:T(8,128)S(1)}) all-reduce(f32[32,32]{0,1:T(8,128)S(1)} %fusion.6, f32[32,32]{0,1:T(8,128)S(1)} %fusion.4), channel_id=1, replica_groups=mesh['rows'=8,'grp'=4] {'rows','grp'}, use_global_device_ids=true, to_apply=%region_10.15 | all-reduce | flops 2048 | bytes 16384 | tf_op jit(solution)/shard_map/psum | solution.py:51
  296.4 0.7 gather_fusion.3
  298.0 2.9 cholesky.282
  301.8 0.6 select_select_fusion.5
  302.7 0.7 copy.105
  303.7 2.9 cholesky.293
  307.3 0.7 select_bitcast_fusion
  308.0 2.4 custom-call.49
  311.0 2.9 cholesky.304
  314.6 0.7 fusion.67
  315.2 2.4 custom-call.48
  318.4 2.9 cholesky.315
  322.0 1.3 select_select_fusion.4
  324.4 1.1 convolution_add_fusion
  (156 shorter events, 30.2 us)
Async XLA Ops:
  0.6 6.4 %copy-start = (f32[32,2048]{1,0:T(8,128)S(1)}, f32[32,2048]{1,0:T(8,128)}, u32[]{:S(2)}) copy-start(f32[32,2048]{1,0:T(8,128)} %param.10) | copy-start | bytes 786436
  2.6 4.4 %copy-start.1 = (f32[32,32]{1,0:T(8,128)S(1)}, f32[32,32]{1,0:T(8,128)}, u32[]{:S(2)}) copy-start(f32[32,32]{1,0:T(8,128)} %param.11) | copy-start | bytes 12292
  2.6 54.5 %all-to-all-start = ((bf16[8,4,2048]{2,0,1:T(8,128)(2,1)}), bf16[8,4,2048]{2,0,1:T(8,128)(2,1)S(1)}, u32[]{:S(2)}, u32[]{:S(2)}) async-start(bf16[8,4,2048]{2,0,1:T(8,128)(2,1)} %bitcast), calls=%async_computation | async-start | bytes 262144 | tf_op jit(solution)/shard_map/all_to_all | solution.py:49
  57.0 60.0 %all-to-all-start.1 = ((bf16[8,4,2048]{2,0,1:T(8,128)(2,1)}), bf16[8,4,2048]{2,0,1:T(8,128)(2,1)S(1)}, u32[]{:S(2)}, u32[]{:S(2)}) async-start(bf16[8,4,2048]{2,0,1:T(8,128)(2,1)} %bitcast.15), calls=%async_computation.1 | async-start | bytes 262144 | tf_op jit(solution)/shard_map/all_to_all | solution.py:49
  117.1 70.6 %all-to-all-start.2 = ((bf16[8,4,2048]{2,0,1:T(8,128)(2,1)}), bf16[8,4,2048]{2,0,1:T(8,128)(2,1)S(1)}, u32[]{:S(2)}, u32[]{:S(2)}) async-start(bf16[8,4,2048]{2,0,1:T(8,128)(2,1)} %bitcast.39), calls=%async_computation.2 | async-start | bytes 262144 | tf_op jit(solution)/shard_map/all_to_all | solution.py:49
  187.7 67.8 %all-to-all-start.3 = ((bf16[8,4,2048]{2,0,1:T(8,128)(2,1)}), bf16[8,4,2048]{2,0,1:T(8,128)(2,1)S(1)}, u32[]{:S(2)}, u32[]{:S(2)}) async-start(bf16[8,4,2048]{2,0,1:T(8,128)(2,1)} %bitcast.63), calls=%async_computation.3 | async-start | bytes 262144 | tf_op jit(solution)/shard_map/all_to_all | solution.py:49
